TPU v7x, 8 devices: a whole 2x2x1 slice. The times are simulated.
8 devices in a mesh: batch: 1 (over z), row: 2 (over y), col: 4 (over x, core).
Axes of the slice: x: 2, y: 2, z: 1, core: 2. Of those that a mesh axis runs over, the one named last changes fastest.
Arguments:
- l_mat: bfloat16 [14336, 14336], P(('batch', 'row'), 'col')
- b_mat: bfloat16 [14336, 8192], P(('batch', 'row'), 'col')
Outputs:
- output: bfloat16 [14336, 8192], P(('batch', 'row'), 'col')
All inputs are finite; a program needn't handle non-finite values.
Results may differ from a plain program's by a relative error of at most 0.001.
Values are sent between devices in bfloat16 or wider.
A program may use at most 1 GiB of HBM per device.

v0:
```python
import jax
import jax.numpy as jnp
from jax import lax
from jax.sharding import PartitionSpec as P


def solution(mesh):
    block_spec = P(('batch', 'row'), 'col')

    def local_product(l_block, b_block):
        l_strip = lax.all_gather(l_block, 'col', axis=1, tiled=True)
        b_strip = lax.all_gather(b_block, 'row', axis=0, tiled=True)
        result = jnp.dot(l_strip, b_strip, preferred_element_type=jnp.float32)
        return result.astype(b_block.dtype)

    return jax.shard_map(local_product, mesh=mesh, in_specs=(block_spec, block_spec), out_specs=block_spec, check_vma=False)
```

profile of v0, /device:TPU:6, one launch (start us, length us, event | category | flops | bytes accessed | tf_op | source)
XLA Modules:
  0.0 2308.4 jit_solution(11556089154670613996)
XLA Ops:
  6.5 0.0 all-gather.5.cloned.1.call-start
  6.5 0.7 all-gather.5.cloned.1.call-update
  7.3 0.0 all-gather.3.cloned.1.call-start
  7.3 0.7 all-gather.3.cloned.1.call-update
  8.0 669.6 %all-gather.5.cloned.1.call-done = bf16[14336,2048]{1,0:T(8,128)(2,1)} async-done(((bf16[7168,2048]{1,0:T(8,128)(2,1)}), bf16[14336,2048]{1,0:T(8,128)(2,1)}) %all-gather.5.cloned.1.call-update) | async-done | bytes 58720272 | tf_op jit(solution)/shard_map/all_gather | solution.py:12
  677.6 1177.9 %all-gather.3.cloned.1.call-done = bf16[7168,14336]{1,0:T(8,128)(2,1)} async-done(((bf16[7168,3584]{1,0:T(8,128)(2,1)}), bf16[7168,14336]{1,0:T(8,128)(2,1)}) %all-gather.3.cloned.1.call-update) | async-done | bytes 205520912 | tf_op jit(solution)/shard_map/all_gather | solution.py:11
  1855.6 446.0 %convolution_convert_fusion = bf16[7168,2048]{1,0:T(8,128)(2,1)} fusion(bf16[7168,14336]{1,0:T(8,128)(2,1)} %all-gather.3.cloned.1.call-done, bf16[14336,2048]{1,0:T(8,128)(2,1)} %all-gather.5.cloned.1.call-done), kind=kOutput, calls=%fused_computation | convolution fusion | flops 420921475072 | bytes 293601280 | tf_op jit(solution)/shard_map/dot_general | solution.py:13
Async XLA Ops:
  6.5 671.1 %all-gather.5.cloned.1.call-start = ((), (), s32[]{:S(2)}) async-start(), calls=%async_computation.1 | async-start | bytes 88080384 | tf_op jit(solution)/shard_map/all_gather | solution.py:12
  7.3 1848.3 %all-gather.3.cloned.1.call-start = ((), (), s32[]{:S(2)}) async-start(), calls=%async_computation | async-start | bytes 256901120 | tf_op jit(solution)/shard_map/all_gather | solution.py:11
Sparse Core Ops, SparseCore 0:
  8.8 668.7 all-gather.4
  679.2 1176.3 all-gather.2
where the time goes:
time: 2310 us
  waiting for transfers between devices  1850 us (80%)
  matrix products  446 us (19%)
    all_gather x1, waiting for transfers between devices, local_product(): l_strip = lax.all_gather(l_block, 'col', axis=1, tiled=True)  1180 us
    all_gather x1, waiting for transfers between devices, local_product(): b_strip = lax.all_gather(b_block, 'row', axis=0, tiled=True)  670 us
    dot_general x1, matrix products, local_product(): result = jnp.dot(l_strip, b_strip, preferred_element_type=jnp.float32)  446 us
  transfers between devices with their start and end apart: 2, of which 2 were waited for; matrix products, arithmetic and copies ran while one was open for 0% of the time, Pallas kernels for 0%

commit v1 on v0

v1 whole, which is shorter than its diff:
```python
import functools

import jax
import jax.numpy as jnp
from jax import lax
from jax.experimental import pallas as pl
from jax.experimental.pallas import tpu as pltpu
from jax.sharding import PartitionSpec as P

MESH = pl.DeviceIdType.MESH
S = 896
KT = 1792
NT = 1024
UNIT = 224
RELAY = 25


def kernel(l_ref, b_ref, x_ref, lap, lbr, lbp, brem, lt, bt, acc, ot,
           lsem, bsem, osem, zsem, gsem, bs, br, ls, lr, ps, pr, qs, qr):
    batch, row, col = lax.axis_index('batch'), lax.axis_index('row'), lax.axis_index('col')
    x, c = col // 2, col % 2
    is_a = (row == 0) & (x == 0)
    is_b = (row == 0) & (x == 1)
    is_c = (row == 1) & (x == 0)
    is_d = (row == 1) & (x == 1)
    half = l_ref.shape[1]
    peer = (batch, row, 2 * x + 1 - c)
    across = (batch, row, 2 * (1 - x) + c)
    along = (batch, 1 - row, col)
    diag = (batch, 1 - row, 2 * (1 - x) + c)

    barrier = pltpu.get_barrier_semaphore()
    for device in (peer, across, along, diag):
        pl.semaphore_signal(barrier, inc=1, device_id=device, device_id_type=MESH)
    pl.semaphore_wait(barrier, 4)

    def remote(src, dst, send, recv, device):
        return pltpu.make_async_remote_copy(
            src_ref=src, dst_ref=dst, send_sem=send, recv_sem=recv,
            device_id=device, device_id_type=MESH)

    def b_copy(n):
        cols = pl.ds(n * NT, NT)
        return remote(b_ref.at[:, cols], brem.at[:, cols], bs.at[n], br.at[n], along)

    def tri_copy(i, h):
        width = min((i + 1) * S - h * half, half)
        rows, cols = pl.ds(i * S, S), pl.ds(0, width)
        return remote(l_ref.at[rows, cols], lbr.at[rows, cols], ls.at[i], lr.at[i], across)

    def full_copy(i):
        rows = pl.ds(i * S, S)
        return remote(l_ref.at[rows], lbr.at[rows], ls.at[i], lr.at[i], across)

    def unit_copy(u, src, device):
        rows = pl.ds(u * UNIT, UNIT)
        return remote(src.at[rows], lbr.at[rows], ls.at[u - 16], lr.at[u - 16], device)

    def la_copy(i):
        rows = pl.ds(i * S, S)
        return remote(l_ref.at[rows], lap.at[rows], ps.at[i], pr.at[i], peer)

    def lb_copy(i):
        rows = pl.ds(i * S, S)
        return remote(lbr.at[rows], lbp.at[rows], qs.at[i], qr.at[i], peer)

    tri_pairs = [(i, h) for h in (0, 1) for i in range(4 * h, 8)]

    def each_tri(do):
        for h in (0, 1):
            @pl.when(c == h)
            def _():
                for i in range(4 * h, 8):
                    do(i, h)

    def each_la(do):
        @pl.when(is_c | (c == 0))
        def _():
            for i in range(4):
                do(i)
        for i in range(4, 8):
            do(i)

    @pl.when(~is_b)
    def _():
        each_la(lambda i: la_copy(i).start())

    @pl.when(row == 0)
    def _():
        for n in range(2):
            b_copy(n).start()

    @pl.when(is_a | is_d)
    def _():
        each_tri(lambda i, h: tri_copy(i, h).start())

    @pl.when(is_c)
    def _():
        for u in list(range(28, 32)) + list(range(RELAY, 28)):
            unit_copy(u, l_ref, along).start()
        unit_copy(24, l_ref, across).start()
        for i in range(6):
            full_copy(i).start()

    @pl.when(is_b | is_c)
    def _():
        ot[0] = jnp.zeros_like(ot[0])
        corners = [
            pltpu.make_async_copy(
                ot.at[0, :, pl.ds(0, S)],
                lbr.at[pl.ds(pl.multiple_of((4 * c + j) * S, S), S), pl.ds((j + 1) * S, S)],
                zsem.at[j // 2])
            for j in (0, 2)]
        for copy in corners:
            copy.start()
        for copy in corners:
            copy.wait()

    def strip_of(r):
        q = r - 8
        i_d = jnp.where(r < 4, r, jnp.where(r < 8, r - 4, jnp.where(q < 2, 4, jnp.where(q < 4, 7, 3 + q // 2))))
        n_d = jnp.where(r < 4, 0, jnp.where(r < 8, 1, q % 2))
        return jnp.where(is_d, i_d, r % 8), jnp.where(is_d, n_d, r // 8)

    def counts(i):
        tri = i // 2 + 1
        na = jnp.where(is_c, 4, jnp.where(is_b, 0, tri))
        nb = jnp.where(is_d, 4, jnp.where(is_a, 0, tri))
        return na, nb

    def own_count(nk):
        first = jnp.minimum(nk, 2)
        return jnp.where(c == 0, first, nk - first)

    def arrive(i, nb_own):
        for k in range(8):
            @pl.when(i == k)
            def _():
                @pl.when(is_d)
                def _():
                    if k < 6:
                        full_copy(k).wait_recv()
                    else:
                        for u in range(4 * k, 4 * k + 4):
                            unit_copy(u, l_ref, across).wait_recv()

                @pl.when(~is_d)
                def _():
                    for h in (0, 1):
                        if k >= 4 * h:
                            @pl.when(c == h)
                            def _():
                                tri_copy(k, h).wait_recv()

                @pl.when(nb_own > 0)
                def _():
                    lb_copy(k).start()

    def fetch(r, t, slot):
        i, n = strip_of(r)
        na, nb = counts(i)
        in_a = t < na
        tt = jnp.where(in_a, t, t - na)
        nk = jnp.where(in_a, na, nb)
        own = own_count(nk)
        mine = tt < own
        kt = jnp.where(mine, 2 * c + tt, 2 * (1 - c) + tt - own)
        first = n == 0

        @pl.when(first & jnp.logical_not(in_a) & (tt == 0))
        def _():
            arrive(i, own)

        @pl.when(first & jnp.logical_not(mine) & (tt == own))
        def _():
            @pl.when(in_a)
            def _():
                la_copy(i).wait_recv()

            @pl.when(jnp.logical_not(in_a))
            def _():
                lb_copy(i).wait_recv()

        use_rem = (is_c & in_a) | (is_d & jnp.logical_not(in_a))

        @pl.when(use_rem & (i == 0) & (tt == 0))
        def _():
            b_copy(n).wait_recv()

        rows = pl.ds(pl.multiple_of(i * S, S), S)
        cols = pl.ds(pl.multiple_of((kt % 2) * KT, KT), KT)
        for pick, ref in (
            (in_a & mine, l_ref),
            (in_a & jnp.logical_not(mine), lap),
            (jnp.logical_not(in_a) & mine, lbr),
            (jnp.logical_not(in_a) & jnp.logical_not(mine), lbp),
        ):
            @pl.when(pick)
            def _():
                pltpu.make_async_copy(ref.at[rows, cols], lt.at[slot], lsem.at[slot]).start()
        depth = pl.ds(pl.multiple_of(kt * KT, KT), KT)
        ncols = pl.ds(pl.multiple_of(n * NT, NT), NT)
        for pick, ref in ((use_rem, brem), (jnp.logical_not(use_rem), b_ref)):
            @pl.when(pick)
            def _():
                pltpu.make_async_copy(ref.at[depth, ncols], bt.at[slot], bsem.at[slot]).start()

    def store(r, slot):
        i, n = strip_of(r)
        rows = pl.ds(pl.multiple_of(i * S, S), S)
        cols = pl.ds(pl.multiple_of(n * NT, NT), NT)
        return pltpu.make_async_copy(ot.at[slot], x_ref.at[rows, cols], osem.at[slot])

    steps = jnp.where(row == 0, 40, 104)
    fetch(jnp.int32(0), jnp.int32(0), 0)

    def step(s, state):
        r, t = state
        i, _ = strip_of(r)
        na, nb = counts(i)
        last = t + 1 == na + nb
        r_next = jnp.where(last, r + 1, r)
        t_next = jnp.where(last, 0, t + 1)
        slot = s % 2

        @pl.when(s + 1 < steps)
        def _():
            fetch(r_next, t_next, 1 - slot)

        @pl.when(t == 0)
        def _():
            acc[...] = jnp.zeros_like(acc)

        pltpu.make_async_copy(l_ref.at[pl.ds(0, S), pl.ds(0, KT)], lt.at[slot], lsem.at[slot]).wait()
        pltpu.make_async_copy(b_ref.at[pl.ds(0, KT), pl.ds(0, NT)], bt.at[slot], bsem.at[slot]).wait()
        acc[...] += jnp.dot(lt[slot], bt[slot], preferred_element_type=jnp.float32)

        @pl.when(last)
        def _():
            oslot = r % 2

            @pl.when(r >= 2)
            def _():
                store(r - 2, oslot).wait()
            ot[oslot] = acc[...].astype(ot.dtype)
            store(r, oslot).start()
        return r_next, t_next

    lax.fori_loop(0, steps, step, (jnp.int32(0), jnp.int32(0)))
    store(jnp.int32(14), 0).wait()
    store(jnp.int32(15), 1).wait()

    relayed = list(range(28, 32)) + list(range(RELAY, 28))

    @pl.when(is_a)
    def _():
        each_tri(lambda i, h: tri_copy(i, h).wait_send())
        for n in range(2):
            b_copy(n).wait_send()
        pl.semaphore_signal(gsem, inc=1, device_id=peer, device_id_type=MESH)
        pl.semaphore_wait(gsem, 1)
        for u in relayed:
            unit_copy(u, lbr, diag).wait_recv()
            unit_copy(u, lbr, diag).start()

    @pl.when(~is_b)
    def _():
        each_la(lambda i: la_copy(i).wait_send())

    @pl.when(is_b)
    def _():
        for n in range(2):
            b_copy(n).wait_send()

    @pl.when(is_d)
    def _():
        each_tri(lambda i, h: tri_copy(i, h).wait_send())

    @pl.when(is_c)
    def _():
        for i in range(6):
            full_copy(i).wait_send()
        unit_copy(24, l_ref, across).wait_send()

    @pl.when(is_c | is_a)
    def _():
        for u in range(RELAY, 32):
            unit_copy(u, l_ref, along).wait_send()

    @pl.when(~is_a)
    def _():
        @pl.when(is_d | (c == 0))
        def _():
            for i in range(4):
                lb_copy(i).wait_send()
        for i in range(4, 8):
            lb_copy(i).wait_send()


def solution(mesh):
    block_spec = P(('batch', 'row'), 'col')

    def local_product(l_block, b_block):
        rows, half = l_block.shape
        columns = b_block.shape[1]
        l_like = jax.ShapeDtypeStruct((rows, half), l_block.dtype)
        b_like = jax.ShapeDtypeStruct((rows, columns), b_block.dtype)
        dma = pltpu.SemaphoreType.DMA
        out = pl.pallas_call(
            kernel,
            out_shape=[b_like, l_like, l_like, l_like, b_like],
            in_specs=[pl.BlockSpec(memory_space=pl.ANY)] * 2,
            out_specs=[pl.BlockSpec(memory_space=pl.ANY)] * 5,
            scratch_shapes=[
                pltpu.VMEM((2, S, KT), l_block.dtype),
                pltpu.VMEM((2, KT, NT), b_block.dtype),
                pltpu.VMEM((S, NT), jnp.float32),
                pltpu.VMEM((2, S, NT), b_block.dtype),
                dma((2,)), dma((2,)), dma((2,)), dma((2,)), pltpu.SemaphoreType.REGULAR,
                dma((2,)), dma((2,)), dma((16,)), dma((16,)),
                dma((8,)), dma((8,)), dma((8,)), dma((8,)),
            ],
            compiler_params=pltpu.CompilerParams(
                collective_id=0, has_side_effects=True, vmem_limit_bytes=48 * 2**20),
            name='triangular_product',
        )(l_block, b_block)
        return out[0]

    return jax.shard_map(local_product, mesh=mesh, in_specs=(block_spec, block_spec),
                         out_specs=block_spec, check_vma=False)
```

time: 2310 us -> 992 us (0.43)
  waiting for transfers between devices: 1850 us -> 0 us
  Pallas kernels: 0 us -> 972 us
  matrix products: 446 us -> 0 us
    all_gather x2 -> x0, waiting for transfers between devices: 1850 us -> none  [the longest x1 1180 us: local_product(): l_strip = lax.all_gather(l_block, 'col', axis=1, tiled=True)]
    pallas_call x0 -> x1, Pallas kernels: none -> 972 us  [local_product(): pl.pallas_call(kernel, out_shape=[b_like, l_like, l_like, l_like, b_like]...]
    dot_general x1 -> x0, matrix products: 446 us -> none  [local_product(): result = jnp.dot(l_strip, b_strip, preferred_element_type=jnp.float32)]
  transfers between devices with their start and end apart: 2 -> 0, of which waited for: 2 -> 0; matrix products, arithmetic and copies ran while one was open for 0% -> 0% of each run, Pallas kernels for 0% -> 0%
where the time goes in v1:
time: 992 us
  Pallas kernels  972 us (98%)
  local copies, waits for them, and re-layouts  20.1 us (2%)
    pallas_call x1, Pallas kernels, local_product(): pl.pallas_call(kernel, out_shape=[b_like, l_like, l_like, l_like, b_like]...  972 us
    unnamed x1, local copies, waits for them, and re-layouts  20.1 us

profile of v1, /device:TPU:6, one launch (start us, length us, event | category | flops | bytes accessed | tf_op | source)
XLA Modules:
  0.0 991.9 jit_solution(10586262676816566440)
XLA Ops:
  0.0 971.9 %triangular_product.1 = (bf16[7168,2048]{1,0:T(8,128)(2,1)}, bf16[7168,3584]{1,0:T(8,128)(2,1)}, bf16[7168,3584]{1,0:T(8,128)(2,1)}, bf16[7168,3584]{1,0:T(8,128)(2,1)}, bf16[7168,2048]{1,0:T(8,128)(2,1)}) custom-call(bf16[7168,3584]{1,0:T(8,128)(2,1)} %l_ref.1, bf16[7168,2048]{1,0:T(8,128)(2,1)} %b_ref.1), custom_call_target="tpu_custom_call" | custom-call | tf_op jit(solution)/shard_map/triangular_product/pallas_call | solution.py:309
  971.9 20.1 %copy.4 = bf16[7168,2048]{1,0:T(8,128)(2,1)} copy(bf16[7168,2048]{1,0:T(8,128)(2,1)} %get-tuple-element.6) | data formatting | bytes 58720256

commit v2 on v0

v2 whole, which is shorter than its diff:
```python
import jax
import jax.numpy as jnp
from jax import lax
from jax.experimental import pallas as pl
from jax.experimental.pallas import tpu as pltpu
from jax.sharding import PartitionSpec as P

MESH = pl.DeviceIdType.MESH
S = 896
KT = 1792
NT = 1024


def kernel(l_ref, b_ref, x_ref, lap, lbr, lbp, brem, xst, lt, bt, acc, ot,
           lsem, bsem, osem, zsem, bs, br, ls, lr, ps, pr, qs, qr, xs, xr):
    batch, row, col = lax.axis_index('batch'), lax.axis_index('row'), lax.axis_index('col')
    x, c = col // 2, col % 2
    is_a = (row == 0) & (x == 0)
    is_b = (row == 0) & (x == 1)
    is_c = (row == 1) & (x == 0)
    is_d = (row == 1) & (x == 1)
    half = l_ref.shape[1]
    peer = (batch, row, 2 * x + 1 - c)
    across = (batch, row, 2 * (1 - x) + c)
    along = (batch, 1 - row, col)

    barrier = pltpu.get_barrier_semaphore()
    for device in (peer, across, along):
        pl.semaphore_signal(barrier, inc=1, device_id=device, device_id_type=MESH)
    pl.semaphore_wait(barrier, 3)

    def remote(src, dst, send, recv, device):
        return pltpu.make_async_remote_copy(
            src_ref=src, dst_ref=dst, send_sem=send, recv_sem=recv,
            device_id=device, device_id_type=MESH)

    def strip(i, lo=0, width=None):
        return pl.ds(i * S, S), pl.ds(lo, half if width is None else width)

    def send_l(src, i, k, out, device, lo=0, width=None):
        return remote(src.at[strip(i, lo, width)], lbr.at[strip(k, lo, width)],
                      ls.at[out], lr.at[k if lo == 0 else 8], device)

    def tri_width(i, h):
        return min((i + 1) * S - h * half, half)

    def send_tri(i, h):
        return send_l(l_ref, i, i, i, across, 0, tri_width(i, h))

    def send_b(n, out, device):
        cols = pl.ds(n * NT, NT)
        return remote(b_ref.at[:, cols], brem.at[:, cols], bs.at[out], br.at[n], device)

    def send_b_top():
        rows = pl.ds(0, KT)
        return remote(b_ref.at[rows], brem.at[rows], bs.at[0], br.at[0], along)

    def send_c(i):
        if i < 2:
            return [send_l(l_ref, i, i, i, along)]
        if i < 7:
            return [send_l(l_ref, i, i, i, across)]
        return [send_l(l_ref, i, i, 7, across, 0, KT), send_l(l_ref, i, i, 8, across, KT, KT)]

    def relay(j):
        return send_l(lbr, j, 4 + j, 8 + j, across)

    def send_l11_top(j):
        return send_l(l_ref, j, 6 + j, 8 + j, along, 0, tri_width(j, 0))

    def la_copy(i):
        rows = pl.ds(i * S, S)
        return remote(l_ref.at[rows], lap.at[rows], ps.at[i], pr.at[i], peer)

    def lb_copy(i, lo=0, width=None):
        at = strip(i, lo, width)
        k = i if lo == 0 else 8
        return remote(lbr.at[at], lbp.at[at], qs.at[k], qr.at[k], peer)

    def send_x(i, n, k):
        cols = pl.ds(pl.multiple_of(n * NT, NT), NT)
        src = pl.ds(pl.multiple_of(i % 4 * S, S), S)
        dst = pl.ds(pl.multiple_of(i * S, S), S)
        target = (batch, jnp.where(is_a, row, 1 - row), jnp.where(is_a, 2 * (1 - x) + c, col))
        return remote(xst.at[src, cols], x_ref.at[dst, cols], xs.at[k], xr.at[k], target)

    def each_tri(do):
        for h in (0, 1):
            @pl.when(c == h)
            def _():
                for i in range(4 * h, 8):
                    do(i, h)

    def each_la(do):
        @pl.when(is_c | (is_a & (c == 0)))
        def _():
            for i in range(2):
                do(i)

        @pl.when(is_c | (c == 0))
        def _():
            for i in range(2, 4):
                do(i)
        for i in range(4, 8):
            do(i)

    def own_sends(do):
        @pl.when(is_a)
        def _():
            for n in range(2):
                do(send_b(n, n, along))

            @pl.when(c == 0)
            def _():
                for i in range(4):
                    do(send_tri(i, 0))

        @pl.when(is_b)
        def _():
            for n in range(2):
                do(send_b(n, n, along))
                do(send_b(n, 2 + n, across))

        @pl.when(is_c)
        def _():
            for i in range(8):
                for copy in send_c(i):
                    do(copy)

        @pl.when(is_d)
        def _():
            @pl.when(c == 0)
            def _():
                for j in range(2):
                    do(send_l11_top(j))
            do(send_b_top())
            each_tri(lambda i, h: do(send_tri(i, h)))

        @pl.when(jnp.logical_not(is_b))
        def _():
            each_la(lambda i: do(la_copy(i)))

    own_sends(lambda copy: copy.start())

    def zero_corner(k, j):
        @pl.when((is_c & (c == k // 4)) | (is_b & (c == 0) & (k != 4)))
        def _():
            cols = pl.ds((1 if k in (0, 4) or j == 6 else 3) * S, S)
            copy = pltpu.make_async_copy(ot.at[:, pl.ds(0, S)], lbr.at[pl.ds(k * S, S), cols], zsem)
            copy.start()
            copy.wait()

    @pl.when(is_b | is_c)
    def _():
        ot[...] = jnp.zeros_like(ot)
        for k in (0, 2, 4):
            zero_corner(k, k)

        @pl.when(is_c & (c == 1))
        def _():
            copy = pltpu.make_async_copy(
                ot.at[:, pl.ds(0, S)], lbr.at[pl.ds(6 * S, S), pl.ds(3 * S, S)], zsem)
            copy.start()
            copy.wait()

        @pl.when(is_b & (c == 0))
        def _():
            copy = pltpu.make_async_copy(
                ot.at[:, pl.ds(0, S)], lbr.at[pl.ds(6 * S, S), pl.ds(S, S)], zsem)
            copy.start()
            copy.wait()

    def pick(a, b, c_, d):
        return jnp.where(is_a, a, jnp.where(is_b, b, jnp.where(is_c, c_, d)))

    def run_of(r):
        late = pick(r >= 16, r >= 8, False, False)
        i = pick(jnp.where(late, 4 + r % 4, r % 8), jnp.where(late, r % 2, r % 4),
                 r % 8, jnp.where(r >= 8, r - 2, 2 + r % 4))
        n = pick(jnp.where(late, (r - 16) // 4, r // 8), jnp.where(late, (r - 8) // 2, r // 4),
                 r // 8, jnp.where(r >= 8, 0, r // 4))
        pair = is_d & (r >= 8)
        tri = i // 2 + 1
        na = pick(tri, 0, 4, tri)
        nb = pick(0, jnp.where(late, 4, tri), tri, 4)
        nc = jnp.where(is_b & late, 1, 0)
        return late, i, n, pair, na, nb, nc

    def place(n, pair, t):
        return jnp.where(pair, t % 2, n), jnp.where(pair, t // 2, t)

    def arrive(k_dyn, own):
        for k in range(8):
            @pl.when(k_dyn == k)
            def _():
                @pl.when(is_d)
                def _():
                    if k < 7:
                        send_l(l_ref, k, k, k, across).wait_recv()
                    else:
                        send_l(l_ref, k, k, k, across, 0, KT).wait_recv()

                @pl.when(is_c)
                def _():
                    for h in (0, 1):
                        if k >= 4 * h:
                            @pl.when(c == h)
                            def _():
                                send_tri(k, h).wait_recv()

                @pl.when(is_b)
                def _():
                    if k in (4, 5):
                        send_l(l_ref, k, k, k, across).wait_recv()
                    else:
                        @pl.when(c == 0)
                        def _():
                            send_l(l_ref, k, k, k, across, 0, tri_width(k % 6, 0)).wait_recv()

                @pl.when(own > 0)
                def _():
                    if k < 7:
                        lb_copy(k).start()
                    else:
                        @pl.when(is_d)
                        def _():
                            lb_copy(k, 0, KT).start()

                        @pl.when(jnp.logical_not(is_d))
                        def _():
                            lb_copy(k).start()

    def wait_peer(k_dyn):
        for k in range(8):
            @pl.when(k_dyn == k)
            def _():
                if k < 7:
                    lb_copy(k).wait_recv()
                else:
                    @pl.when(is_d)
                    def _():
                        lb_copy(k, 0, KT).wait_recv()

                    @pl.when(jnp.logical_not(is_d))
                    def _():
                        lb_copy(k).wait_recv()

    def fetch(r, t, slot):
        late, i, n_run, pair, na, nb, nc = run_of(r)
        n, tt = place(n_run, pair, t)
        in_a = tt < na
        in_c = tt >= na + nb
        in_b = jnp.logical_not(in_a) & jnp.logical_not(in_c)
        u = jnp.where(in_a, tt, jnp.where(in_c, tt - na - nb, tt - na))
        nk = jnp.where(in_a, na, jnp.where(in_c, nc, nb))
        full = (is_c & in_a) | (is_d & in_b) | (is_b & late & in_b)
        low = jnp.minimum(nk, 2)
        own = jnp.where(c == 0, low, nk - low)
        mine = (full & (u % 2 == 0)) | (jnp.logical_not(full) & (u < own))
        idx = jnp.where(full, u // 2, jnp.where(mine, u, u - own))
        kt = jnp.where(mine, 2 * c, 2 * (1 - c)) + idx
        k_strip = jnp.where(is_b & late, jnp.where(in_c, 6 + i, 4 + i), i)
        first = (n == 0) & jnp.logical_not(is_a & late)
        split = is_d & (i == 7)

        @pl.when(first & jnp.logical_not(in_a) & (u == 0))
        def _():
            with jax.named_scope('wait_rail'):
                arrive(k_strip, own)

        @pl.when(first & in_b & split & (u == 2))
        def _():
            with jax.named_scope('wait_rail_last'):
                send_l(l_ref, 7, 7, 8, across, KT, KT).wait_recv()
                lb_copy(7, KT, KT).start()

        @pl.when(first & jnp.logical_not(mine) & (idx == 0))
        def _():
            with jax.named_scope('wait_peer'):
                @pl.when(in_a)
                def _():
                    la_copy(i).wait_recv()

                @pl.when(jnp.logical_not(in_a))
                def _():
                    wait_peer(k_strip)

        @pl.when(first & in_b & split & (u == 3))
        def _():
            lb_copy(7, KT, KT).wait_recv()

        @pl.when(is_a & late & (i == 4) & (n == 0) & (u == 0))
        def _():
            with jax.named_scope('relay'):
                for j in range(2):
                    send_l(l_ref, j, j, j, along).wait_recv()
                    relay(j).start()

        @pl.when(((is_a & late & (i == 4)) | (is_c & in_a & (i == 0)) | (is_d & in_b & (i == 2))) & (u == 0))
        def _():
            with jax.named_scope('wait_b'):
                send_b(n, n, along).wait_recv()

        @pl.when(in_c & (i == 0) & (n == 0))
        def _():
            with jax.named_scope('wait_b'):
                send_b_top().wait_recv()

        use_rem = (is_a & late) | (is_c & in_a) | (is_d & in_b) | in_c
        rows = pl.ds(pl.multiple_of(k_strip * S, S), S)
        cols = pl.ds(pl.multiple_of((kt % 2) * KT, KT), KT)
        for take, ref in (
            (in_a & mine, l_ref),
            (in_a & jnp.logical_not(mine), lap),
            (jnp.logical_not(in_a) & mine, lbr),
            (jnp.logical_not(in_a) & jnp.logical_not(mine), lbp),
        ):
            @pl.when(take)
            def _():
                pltpu.make_async_copy(ref.at[rows, cols], lt.at[slot], lsem.at[slot]).start()
        depth = pl.ds(pl.multiple_of(kt * KT, KT), KT)
        ncols = pl.ds(pl.multiple_of(n * NT, NT), NT)
        for take, ref in ((use_rem, brem), (jnp.logical_not(use_rem), b_ref)):
            @pl.when(take)
            def _():
                pltpu.make_async_copy(ref.at[depth, ncols], bt.at[slot], bsem.at[slot]).start()

    def finish(r, n):
        late, i, _, _, _, _, _ = run_of(r)
        pltpu.make_async_copy(ot, x_ref.at[pl.ds(0, S), pl.ds(0, NT)], osem).wait()

        @pl.when(late)
        def _():
            send_x(i, n, jnp.where(is_a, r - 16, r - 8)).start()

    steps = pick(68, 32, 104, 84)
    fetch(jnp.int32(0), jnp.int32(0), 0)

    def step(s, state):
        r, t, waiting, r_old, n_old = state
        late, i, n_run, pair, na, nb, nc = run_of(r)
        n, tt = place(n_run, pair, t)
        total = na + nb + nc
        ends = t + 1 == jnp.where(pair, 2 * total, total)
        r_next = jnp.where(ends, r + 1, r)
        t_next = jnp.where(ends, 0, t + 1)
        slot = s % 2
        last = tt + 1 == total

        @pl.when(s + 1 < steps)
        def _():
            fetch(r_next, t_next, 1 - slot)

        @pl.when(tt == 0)
        def _():
            acc[n] = jnp.zeros_like(acc[n])

        pltpu.make_async_copy(l_ref.at[pl.ds(0, S), pl.ds(0, KT)], lt.at[slot], lsem.at[slot]).wait()
        pltpu.make_async_copy(b_ref.at[pl.ds(0, KT), pl.ds(0, NT)], bt.at[slot], bsem.at[slot]).wait()
        with jax.named_scope('dot'):
            acc[n] += jnp.dot(lt[slot], bt[slot], preferred_element_type=jnp.float32)

        @pl.when(waiting == 1)
        def _():
            finish(r_old, n_old)

        @pl.when(last)
        def _():
            ot[...] = acc[n].astype(ot.dtype)
            rows = pl.ds(pl.multiple_of(i * S, S), S)
            staged = pl.ds(pl.multiple_of(i % 4 * S, S), S)
            cols = pl.ds(pl.multiple_of(n * NT, NT), NT)

            @pl.when(late)
            def _():
                pltpu.make_async_copy(ot, xst.at[staged, cols], osem).start()

            @pl.when(jnp.logical_not(late))
            def _():
                pltpu.make_async_copy(ot, x_ref.at[rows, cols], osem).start()
        return r_next, t_next, jnp.where(last, 1, 0), r, n

    zero = jnp.int32(0)
    state = lax.fori_loop(0, steps, step, (zero, zero, zero, zero, zero))
    finish(state[3], state[4])

    @pl.when(is_a)
    def _():
        for j in range(2):
            relay(j).wait_send()
        for k in range(8):
            send_x(4 + k % 4, k // 4, k).wait_send()

    @pl.when(is_b)
    def _():
        with jax.named_scope('wait_x_sent'):
            for k in range(4):
                send_x(k % 2, k // 2, k).wait_send()
        with jax.named_scope('wait_x_in'):
            for k in range(8):
                send_x(4 + k % 4, k // 4, k).wait_recv()

    @pl.when(is_d)
    def _():
        with jax.named_scope('wait_x_in'):
            for k in range(4):
                send_x(k % 2, k // 2, k).wait_recv()

    with jax.named_scope('wait_own_sends'):
        own_sends(lambda copy: copy.wait_send())

    @pl.when(jnp.logical_not(is_a))
    def _():
        @pl.when(is_b)
        def _():
            for k in (4, 5):
                lb_copy(k).wait_send()

            @pl.when(c == 0)
            def _():
                for k in (0, 1, 2, 3, 6, 7):
                    lb_copy(k).wait_send()

        @pl.when(is_c)
        def _():
            @pl.when(c == 0)
            def _():
                for k in range(4):
                    lb_copy(k).wait_send()
            for k in range(4, 8):
                lb_copy(k).wait_send()

        @pl.when(is_d)
        def _():
            for k in range(2, 7):
                lb_copy(k).wait_send()
            lb_copy(7, 0, KT).wait_send()
            lb_copy(7, KT, KT).wait_send()


def solution(mesh):
    block_spec = P(('batch', 'row'), 'col')

    def local_product(l_block, b_block):
        rows, half = l_block.shape
        columns = b_block.shape[1]
        l_like = jax.ShapeDtypeStruct((rows, half), l_block.dtype)
        b_like = jax.ShapeDtypeStruct((rows, columns), b_block.dtype)
        x_like = jax.ShapeDtypeStruct((rows // 2, columns), b_block.dtype)
        dma = pltpu.SemaphoreType.DMA
        out = pl.pallas_call(
            kernel,
            out_shape=[b_like, l_like, l_like, l_like, b_like, x_like],
            in_specs=[pl.BlockSpec(memory_space=pl.ANY)] * 2,
            out_specs=[pl.BlockSpec(memory_space=pl.ANY)] * 6,
            scratch_shapes=[
                pltpu.VMEM((2, S, KT), l_block.dtype),
                pltpu.VMEM((2, KT, NT), b_block.dtype),
                pltpu.VMEM((2, S, NT), jnp.float32),
                pltpu.VMEM((S, NT), b_block.dtype),
                dma((2,)), dma((2,)), dma, dma,
                dma((4,)), dma((2,)), dma((10,)), dma((9,)),
                dma((8,)), dma((8,)), dma((9,)), dma((9,)), dma((8,)), dma((8,)),
            ],
            compiler_params=pltpu.CompilerParams(
                collective_id=0, has_side_effects=True, vmem_limit_bytes=48 * 2**20),
            name='triangular_product',
        )(l_block, b_block)
        return out[0]

    return jax.shard_map(local_product, mesh=mesh, in_specs=(block_spec, block_spec),
                         out_specs=block_spec, check_vma=False)
```

time: 2310 us -> 874 us (0.38)
  waiting for transfers between devices: 1850 us -> 0 us
  Pallas kernels: 0 us -> 851 us
  matrix products: 446 us -> 0 us
    all_gather x2 -> x0, waiting for transfers between devices: 1850 us -> none  [the longest x1 1180 us: local_product(): l_strip = lax.all_gather(l_block, 'col', axis=1, tiled=True)]
    pallas_call x0 -> x1, Pallas kernels: none -> 851 us  [local_product(): pl.pallas_call(kernel, out_shape=[b_like, l_like, l_like, l_like, b_like,...]
    dot_general x1 -> x0, matrix products: 446 us -> none  [local_product(): result = jnp.dot(l_strip, b_strip, preferred_element_type=jnp.float32)]
  transfers between devices with their start and end apart: 2 -> 0, of which waited for: 2 -> 0; matrix products, arithmetic and copies ran while one was open for 0% -> 0% of each run, Pallas kernels for 0% -> 0%
where the time goes in v2:
time: 874 us; the launch traced here: 871 us
  Pallas kernels  851 us (97%)
  local copies, waits for them, and re-layouts  20.1 us (2%)
    pallas_call x1, Pallas kernels, local_product(): pl.pallas_call(kernel, out_shape=[b_like, l_like, l_like, l_like, b_like,...  851 us
    unnamed x1, local copies, waits for them, and re-layouts  20.1 us

profile of v2, /device:TPU:6, one launch (start us, length us, event | category | flops | bytes accessed | tf_op | source)
XLA Modules:
  0.0 871.3 jit_solution(9626904603196065279)
XLA Ops:
  0.0 851.2 %triangular_product.1 = (bf16[7168,2048]{1,0:T(8,128)(2,1)}, bf16[7168,3584]{1,0:T(8,128)(2,1)}, bf16[7168,3584]{1,0:T(8,128)(2,1)}, bf16[7168,3584]{1,0:T(8,128...) custom-call(bf16[7168,3584]{1,0:T(8,128)(2,1)} %l_ref.1, bf16[7168,2048]{1,0:T(8,128)(2,1)} %b_ref.1), custom_call_target="tpu_custom_call" | custom-call | tf_op jit(solution)/shard_map/triangular_product/pallas_call | solution.py:451
  851.2 20.1 %copy.4 = bf16[7168,2048]{1,0:T(8,128)(2,1)} copy(bf16[7168,2048]{1,0:T(8,128)(2,1)} %get-tuple-element.6) | data formatting | bytes 58720256

commit v3 on v2

--- a/solution.py
+++ b/solution.py
@@ -9,10 +9,11 @@
 S = 896
 KT = 1792
 NT = 1024
-
-
-def kernel(l_ref, b_ref, x_ref, lap, lbr, lbp, brem, xst, lt, bt, acc, ot,
-           lsem, bsem, osem, zsem, bs, br, ls, lr, ps, pr, qs, qr, xs, xr):
+Q = 224
+
+
+def kernel(l_ref, b_ref, x_ref, lap, lbr, lbp, brem, xst, pst, lt, bt, acc, ot,
+           lsem, bsem, osem, psem, zsem, bs, br, ls, lr, ps, pr, qs, qr, xs, xr):
     batch, row, col = lax.axis_index('batch'), lax.axis_index('row'), lax.axis_index('col')
     x, c = col // 2, col % 2
     is_a = (row == 0) & (x == 0)
@@ -51,21 +52,33 @@
         cols = pl.ds(n * NT, NT)
         return remote(b_ref.at[:, cols], brem.at[:, cols], bs.at[out], br.at[n], device)
 
-    def send_b_top():
-        rows = pl.ds(0, KT)
-        return remote(b_ref.at[rows], brem.at[rows], bs.at[0], br.at[0], along)
+    def send_b_top(j):
+        rows = pl.ds(j * KT, KT)
+        return remote(b_ref.at[rows], brem.at[rows], bs.at[j], br.at[j], along)
+
+    def send_rows(src, at, to, rows, k, out, device):
+        return remote(src.at[pl.ds(at, rows)], lbr.at[pl.ds(to, rows)], ls.at[out], lr.at[k], device)
+
+    def send_rest():
+        return send_rows(l_ref, 2 * S + Q, 2 * S + Q, S - Q, 2, 9, across)
 
     def send_c(i):
         if i < 2:
             return [send_l(l_ref, i, i, i, along)]
+        if i == 2:
+            return [send_rows(l_ref, 2 * S, 2 * S, Q, 2, 2, along), send_rest()]
         if i < 7:
             return [send_l(l_ref, i, i, i, across)]
         return [send_l(l_ref, i, i, 7, across, 0, KT), send_l(l_ref, i, i, 8, across, KT, KT)]
 
     def relay(j):
+        if j == 2:
+            return send_rows(lbr, 2 * S, 8 * S, Q, 8, 10, across)
         return send_l(lbr, j, 4 + j, 8 + j, across)
 
     def send_l11_top(j):
+        if j == 2:
+            return send_rows(l_ref, 2 * S, 9 * S, Q, 9, 10, along)
         return send_l(l_ref, j, 6 + j, 8 + j, along, 0, tri_width(j, 0))
 
     def la_copy(i):
@@ -84,6 +97,15 @@
         target = (batch, jnp.where(is_a, row, 1 - row), jnp.where(is_a, 2 * (1 - x) + c, col))
         return remote(xst.at[src, cols], x_ref.at[dst, cols], xs.at[k], xr.at[k], target)
 
+    def send_x_head(n, k):
+        cols = pl.ds(pl.multiple_of(n * NT, NT), NT)
+        at = (pl.ds(2 * S, Q), cols)
+        return remote(xst.at[at], x_ref.at[at], xs.at[k], xr.at[k], along)
+
+    def send_tile_b(k):
+        j, n = k % 3, k // 3
+        return send_x_head(n, k) if j == 2 else send_x(j, n, k)
+
     def each_tri(do):
         for h in (0, 1):
             @pl.when(c == h)
@@ -131,9 +153,10 @@
         def _():
             @pl.when(c == 0)
             def _():
-                for j in range(2):
+                for j in range(3):
                     do(send_l11_top(j))
-            do(send_b_top())
+            for j in range(2):
+                do(send_b_top(j))
             each_tri(lambda i, h: do(send_tri(i, h)))
 
         @pl.when(jnp.logical_not(is_b))
@@ -175,16 +198,28 @@
 
     def run_of(r):
         late = pick(r >= 16, r >= 8, False, False)
-        i = pick(jnp.where(late, 4 + r % 4, r % 8), jnp.where(late, r % 2, r % 4),
-                 r % 8, jnp.where(r >= 8, r - 2, 2 + r % 4))
-        n = pick(jnp.where(late, (r - 16) // 4, r // 8), jnp.where(late, (r - 8) // 2, r // 4),
-                 r // 8, jnp.where(r >= 8, 0, r // 4))
-        pair = is_d & (r >= 8)
+        part = pick(False, False, (r < 3) | ((r >= 6) & (r < 14) & (r % 2 == 1)), r < 8)
+        rest = pick(False, False, (r >= 15) & (r < 22), r >= 12)
+        pair = is_d & (r >= 16)
+        i_c = jnp.where(r < 3, r, jnp.where(r < 6, r - 3, jnp.where(
+            r < 15, r // 2, jnp.where(r < 22, r - 15, 7))))
+        n_c = jnp.where(r < 3, 1, jnp.where(r < 6, 0, jnp.where(r < 15, r % 2, 1)))
+        i_d = jnp.where(r < 4, 2 + r, jnp.where(r < 8, 4 + r // 2, jnp.where(r < 16, 2 + r % 4, r - 10)))
+        n_d = jnp.where(r < 4, 1, jnp.where(r < 8, r % 2, jnp.where(r < 12, 0, jnp.where(r < 16, 1, 0))))
+        i = pick(jnp.where(late, 4 + r % 4, r % 8), jnp.where(late, (r - 8) % 3, r % 4), i_c, i_d)
+        n = pick(jnp.where(late, (r - 16) // 4, r // 8), jnp.where(late, (r - 8) // 3, r // 4), n_c, n_d)
         tri = i // 2 + 1
-        na = pick(tri, 0, 4, tri)
-        nb = pick(0, jnp.where(late, 4, tri), tri, 4)
-        nc = jnp.where(is_b & late, 1, 0)
-        return late, i, n, pair, na, nb, nc
+        na = pick(tri, 0, jnp.where(part, 0, 4), jnp.where(rest, 0, tri))
+        nb = pick(0, jnp.where(late, 4, tri), jnp.where(rest, 0, tri), jnp.where(part, 0, 4))
+        nc = jnp.where(is_b & late, 1 + i // 2, 0)
+        return late, part, rest, i, n, pair, na, nb, nc
+
+    def kept(r, i, n):
+        k = jnp.where(is_c, i, jnp.where(r < 8, r, jnp.where(r < 16, r - 12, 2 * i - 8 + n)))
+        return pst.at[pl.ds(pl.multiple_of(k * S, S), S)]
+
+    def acc_of(r, pair, n):
+        return jnp.where(pair, n, r % 2)
 
     def place(n, pair, t):
         return jnp.where(pair, t % 2, n), jnp.where(pair, t // 2, t)
@@ -195,7 +230,9 @@
             def _():
                 @pl.when(is_d)
                 def _():
-                    if k < 7:
+                    if k == 2:
+                        send_rest().wait_recv()
+                    elif k < 7:
                         send_l(l_ref, k, k, k, across).wait_recv()
                     else:
                         send_l(l_ref, k, k, k, across, 0, KT).wait_recv()
@@ -217,6 +254,17 @@
                         def _():
                             send_l(l_ref, k, k, k, across, 0, tri_width(k % 6, 0)).wait_recv()
 
+                pass_on(k, own)
+
+        @pl.when(is_b)
+        def _():
+            for k in (8, 9):
+                @pl.when((k_dyn == k) & (own > 0))
+                def _():
+                    send_rows(l_ref, 0, k * S, Q, k, 0, across).wait_recv()
+                    lb_copy(k).start()
+
+    def pass_on(k, own):
                 @pl.when(own > 0)
                 def _():
                     if k < 7:
@@ -231,6 +279,13 @@
                             lb_copy(k).start()
 
     def wait_peer(k_dyn):
+        @pl.when(is_b)
+        def _():
+            for k in (8, 9):
+                @pl.when(k_dyn == k)
+                def _():
+                    lb_copy(k).wait_recv()
+
         for k in range(8):
             @pl.when(k_dyn == k)
             def _():
@@ -246,7 +301,7 @@
                         lb_copy(k).wait_recv()
 
     def fetch(r, t, slot):
-        late, i, n_run, pair, na, nb, nc = run_of(r)
+        late, _, rest, i, n_run, pair, na, nb, nc = run_of(r)
         n, tt = place(n_run, pair, t)
         in_a = tt < na
         in_c = tt >= na + nb
@@ -259,8 +314,11 @@
         mine = (full & (u % 2 == 0)) | (jnp.logical_not(full) & (u < own))
         idx = jnp.where(full, u // 2, jnp.where(mine, u, u - own))
         kt = jnp.where(mine, 2 * c, 2 * (1 - c)) + idx
-        k_strip = jnp.where(is_b & late, jnp.where(in_c, 6 + i, 4 + i), i)
-        first = (n == 0) & jnp.logical_not(is_a & late)
+        k_strip = jnp.where(is_b & late, jnp.where(
+            i == 2, jnp.where(in_c, 9, 8), jnp.where(in_c, 6 + i, 4 + i)), i)
+        first = pick((n == 0) & jnp.logical_not(late), n == 0,
+                     (in_a & (n == 0)) | (jnp.logical_not(in_a) & ((r < 3) | ((r >= 6) & (r < 15) & (r % 2 == 0)))),
+                     jnp.where(in_a, (r < 5) | (r == 6), n == 0))
         split = is_d & (i == 7)
 
         @pl.when(first & jnp.logical_not(in_a) & (u == 0))
@@ -292,8 +350,8 @@
         @pl.when(is_a & late & (i == 4) & (n == 0) & (u == 0))
         def _():
             with jax.named_scope('relay'):
-                for j in range(2):
-                    send_l(l_ref, j, j, j, along).wait_recv()
+                for j in range(3):
+                    send_c(j)[0].wait_recv()
                     relay(j).start()
 
         @pl.when(((is_a & late & (i == 4)) | (is_c & in_a & (i == 0)) | (is_d & in_b & (i == 2))) & (u == 0))
@@ -301,10 +359,16 @@
             with jax.named_scope('wait_b'):
                 send_b(n, n, along).wait_recv()
 
-        @pl.when(in_c & (i == 0) & (n == 0))
-        def _():
-            with jax.named_scope('wait_b'):
-                send_b_top().wait_recv()
+        for j in range(2):
+            @pl.when(in_c & (i == 2 * j) & (n == 0) & (u == 0))
+            def _():
+                with jax.named_scope('wait_b'):
+                    send_b_top(j).wait_recv()
+
+        @pl.when(rest & (tt == 0))
+        def _():
+            k = acc_of(r, pair, n)
+            pltpu.make_async_copy(kept(r, i, n), acc.at[k], psem.at[k]).start()
 
         use_rem = (is_a & late) | (is_c & in_a) | (is_d & in_b) | in_c
         rows = pl.ds(pl.multiple_of(k_strip * S, S), S)
@@ -326,19 +390,35 @@
                 pltpu.make_async_copy(ref.at[depth, ncols], bt.at[slot], bsem.at[slot]).start()
 
     def finish(r, n):
-        late, i, _, _, _, _, _ = run_of(r)
-        pltpu.make_async_copy(ot, x_ref.at[pl.ds(0, S), pl.ds(0, NT)], osem).wait()
-
-        @pl.when(late)
+        late, part, _, i, _, _, _, _, _ = run_of(r)
+        head = is_d & (i == 2) & jnp.logical_not(part)
+
+        @pl.when(part)
+        def _():
+            pltpu.make_async_copy(acc.at[0], pst.at[pl.ds(0, S)], osem).wait()
+
+        @pl.when(head)
+        def _():
+            pltpu.make_async_copy(ot.at[pl.ds(Q, S - Q)], x_ref.at[pl.ds(0, S - Q), pl.ds(0, NT)], osem).wait()
+
+        @pl.when(jnp.logical_not(part | head))
+        def _():
+            pltpu.make_async_copy(ot, x_ref.at[pl.ds(0, S), pl.ds(0, NT)], osem).wait()
+
+        @pl.when(late & is_b & (i == 2))
+        def _():
+            send_x_head(n, r - 8).start()
+
+        @pl.when(late & jnp.logical_not(is_b & (i == 2)))
         def _():
             send_x(i, n, jnp.where(is_a, r - 16, r - 8)).start()
 
-    steps = pick(68, 32, 104, 84)
+    steps = pick(68, 44, 104, 84)
     fetch(jnp.int32(0), jnp.int32(0), 0)
 
     def step(s, state):
         r, t, waiting, r_old, n_old = state
-        late, i, n_run, pair, na, nb, nc = run_of(r)
+        late, part, rest, i, n_run, pair, na, nb, nc = run_of(r)
         n, tt = place(n_run, pair, t)
         total = na + nb + nc
         ends = t + 1 == jnp.where(pair, 2 * total, total)
@@ -346,39 +426,67 @@
         t_next = jnp.where(ends, 0, t + 1)
         slot = s % 2
         last = tt + 1 == total
-
-        @pl.when(s + 1 < steps)
+        k = acc_of(r, pair, n)
+        late_old = pick(r_old >= 16, r_old >= 8, False, False)
+
+        @pl.when((waiting == 1) & late_old)
+        def _():
+            finish(r_old, n_old)
+
+        stalls = (is_a & (r_next == 20) & (t_next == 0)) | (is_d & (r_next == 17) & (t_next == 4))
+
+        @pl.when((s + 1 < steps) & jnp.logical_not(stalls))
         def _():
             fetch(r_next, t_next, 1 - slot)
 
-        @pl.when(tt == 0)
-        def _():
-            acc[n] = jnp.zeros_like(acc[n])
+        @pl.when((tt == 0) & rest)
+        def _():
+            pltpu.make_async_copy(pst.at[pl.ds(0, S)], acc.at[k], psem.at[k]).wait()
+
+        @pl.when((tt == 0) & jnp.logical_not(rest))
+        def _():
+            acc[k] = jnp.zeros_like(acc[k])
 
         pltpu.make_async_copy(l_ref.at[pl.ds(0, S), pl.ds(0, KT)], lt.at[slot], lsem.at[slot]).wait()
         pltpu.make_async_copy(b_ref.at[pl.ds(0, KT), pl.ds(0, NT)], bt.at[slot], bsem.at[slot]).wait()
         with jax.named_scope('dot'):
-            acc[n] += jnp.dot(lt[slot], bt[slot], preferred_element_type=jnp.float32)
-
-        @pl.when(waiting == 1)
+            acc[k] += jnp.dot(lt[slot], bt[slot], preferred_element_type=jnp.float32)
+
+        @pl.when((waiting == 1) & jnp.logical_not(late_old))
         def _():
             finish(r_old, n_old)
 
-        @pl.when(last)
-        def _():
-            ot[...] = acc[n].astype(ot.dtype)
+        @pl.when(last & part)
+        def _():
+            pltpu.make_async_copy(acc.at[k], kept(r, i, n), osem).start()
+
+        @pl.when(last & jnp.logical_not(part))
+        def _():
+            ot[...] = acc[k].astype(ot.dtype)
             rows = pl.ds(pl.multiple_of(i * S, S), S)
             staged = pl.ds(pl.multiple_of(i % 4 * S, S), S)
             cols = pl.ds(pl.multiple_of(n * NT, NT), NT)
+            head = is_d & (i == 2)
 
             @pl.when(late)
             def _():
                 pltpu.make_async_copy(ot, xst.at[staged, cols], osem).start()
 
-            @pl.when(jnp.logical_not(late))
+            @pl.when(head)
+            def _():
+                pltpu.make_async_copy(
+                    ot.at[pl.ds(Q, S - Q)], x_ref.at[pl.ds(2 * S + Q, S - Q), cols], osem).start()
+
+            @pl.when(jnp.logical_not(late | head))
             def _():
                 pltpu.make_async_copy(ot, x_ref.at[rows, cols], osem).start()
-        return r_next, t_next, jnp.where(last, 1, 0), r, n
+        @pl.when(stalls)
+        def _():
+            @pl.when(last)
+            def _():
+                finish(r, n)
+            fetch(r_next, t_next, 1 - slot)
+        return r_next, t_next, jnp.where(last & jnp.logical_not(stalls), 1, 0), r, n
 
     zero = jnp.int32(0)
     state = lax.fori_loop(0, steps, step, (zero, zero, zero, zero, zero))
@@ -386,25 +494,25 @@
 
     @pl.when(is_a)
     def _():
-        for j in range(2):
+        for j in range(3):
             relay(j).wait_send()
         for k in range(8):
             send_x(4 + k % 4, k // 4, k).wait_send()
 
     @pl.when(is_b)
     def _():
+        for k in range(8):
+            with jax.named_scope('wait_x_in'):
+                send_x(4 + k % 4, k // 4, k).wait_recv()
         with jax.named_scope('wait_x_sent'):
-            for k in range(4):
-                send_x(k % 2, k // 2, k).wait_send()
-        with jax.named_scope('wait_x_in'):
-            for k in range(8):
-                send_x(4 + k % 4, k // 4, k).wait_recv()
+            for k in range(6):
+                send_tile_b(k).wait_send()
 
     @pl.when(is_d)
     def _():
         with jax.named_scope('wait_x_in'):
-            for k in range(4):
-                send_x(k % 2, k // 2, k).wait_recv()
+            for k in range(6):
+                send_tile_b(k).wait_recv()
 
     with jax.named_scope('wait_own_sends'):
         own_sends(lambda copy: copy.wait_send())
@@ -413,12 +521,12 @@
     def _():
         @pl.when(is_b)
         def _():
-            for k in (4, 5):
+            for k in (4, 5, 8):
                 lb_copy(k).wait_send()
 
             @pl.when(c == 0)
             def _():
-                for k in (0, 1, 2, 3, 6, 7):
+                for k in (0, 1, 2, 3, 6, 7, 9):
                     lb_copy(k).wait_send()
 
         @pl.when(is_c)
@@ -445,22 +553,24 @@
         rows, half = l_block.shape
         columns = b_block.shape[1]
         l_like = jax.ShapeDtypeStruct((rows, half), l_block.dtype)
+        l_more = jax.ShapeDtypeStruct((rows + 2 * S, half), l_block.dtype)
         b_like = jax.ShapeDtypeStruct((rows, columns), b_block.dtype)
         x_like = jax.ShapeDtypeStruct((rows // 2, columns), b_block.dtype)
+        part_like = jax.ShapeDtypeStruct((8 * S, NT), jnp.float32)
         dma = pltpu.SemaphoreType.DMA
         out = pl.pallas_call(
             kernel,
-            out_shape=[b_like, l_like, l_like, l_like, b_like, x_like],
+            out_shape=[b_like, l_like, l_more, l_more, b_like, x_like, part_like],
             in_specs=[pl.BlockSpec(memory_space=pl.ANY)] * 2,
-            out_specs=[pl.BlockSpec(memory_space=pl.ANY)] * 6,
+            out_specs=[pl.BlockSpec(memory_space=pl.ANY)] * 7,
             scratch_shapes=[
                 pltpu.VMEM((2, S, KT), l_block.dtype),
                 pltpu.VMEM((2, KT, NT), b_block.dtype),
                 pltpu.VMEM((2, S, NT), jnp.float32),
                 pltpu.VMEM((S, NT), b_block.dtype),
-                dma((2,)), dma((2,)), dma, dma,
-                dma((4,)), dma((2,)), dma((10,)), dma((9,)),
-                dma((8,)), dma((8,)), dma((9,)), dma((9,)), dma((8,)), dma((8,)),
+                dma((2,)), dma((2,)), dma, dma((2,)), dma,
+                dma((4,)), dma((2,)), dma((11,)), dma((10,)),
+                dma((8,)), dma((8,)), dma((10,)), dma((10,)), dma((8,)), dma((8,)),
             ],
             compiler_params=pltpu.CompilerParams(
                 collective_id=0, has_side_effects=True, vmem_limit_bytes=48 * 2**20),

time: 874 us -> 834 us (0.954)
  Pallas kernels: 851 us -> 814 us
    pallas_call x1, Pallas kernels: 851 us -> 814 us  [local_product(): pl.pallas_call(kernel, out_shape=[b_like, l_like, l_more, l_more, b_like,...]
where the time goes in v3:
time: 834 us
  Pallas kernels  814 us (98%)
  local copies, waits for them, and re-layouts  20.1 us (2%)
    pallas_call x1, Pallas kernels, local_product(): pl.pallas_call(kernel, out_shape=[b_like, l_like, l_more, l_more, b_like,...  814 us
    unnamed x1, local copies, waits for them, and re-layouts  20.1 us

profile of v3, /device:TPU:6, one launch (start us, length us, event | category | flops | bytes accessed | tf_op | source)
XLA Modules:
  0.0 834.3 jit_solution(17524152374999056179)
XLA Ops:
  0.0 814.2 %triangular_product.1 = (bf16[7168,2048]{1,0:T(8,128)(2,1)}, bf16[7168,3584]{1,0:T(8,128)(2,1)}, bf16[8960,3584]{1,0:T(8,128)(2,1)}, bf16[8960,3584]{1,0:T(8,128...) custom-call(bf16[7168,3584]{1,0:T(8,128)(2,1)} %l_ref.1, ...), custom_call_target="tpu_custom_call" | custom-call | tf_op jit(solution)/shard_map/triangular_product/pallas_call | solution.py:561
  814.2 20.1 %copy.4 = bf16[7168,2048]{1,0:T(8,128)(2,1)} copy(bf16[7168,2048]{1,0:T(8,128)(2,1)} %get-tuple-element.6) | data formatting | bytes 58720256

commit v4 on v3

--- a/solution.py
+++ b/solution.py
@@ -9,7 +9,7 @@
 S = 896
 KT = 1792
 NT = 1024
-Q = 224
+Q = 240
 
 
 def kernel(l_ref, b_ref, x_ref, lap, lbr, lbp, brem, xst, pst, lt, bt, acc, ot,

time: 834 us -> 832 us (level)
  no operation moved by 1% of the time
where the time goes in v4:
time: 832 us
  Pallas kernels  812 us (98%)
  local copies, waits for them, and re-layouts  20.1 us (2%)
    pallas_call x1, Pallas kernels, local_product(): pl.pallas_call(kernel, out_shape=[b_like, l_like, l_more, l_more, b_like,...  812 us
    unnamed x1, local copies, waits for them, and re-layouts  20.1 us

profile of v4, /device:TPU:6, one launch (start us, length us, event | category | flops | bytes accessed | tf_op | source)
XLA Modules:
  0.0 831.8 jit_solution(10156761164646536414)
XLA Ops:
  0.0 811.8 %triangular_product.1 = (bf16[7168,2048]{1,0:T(8,128)(2,1)}, bf16[7168,3584]{1,0:T(8,128)(2,1)}, bf16[8960,3584]{1,0:T(8,128)(2,1)}, bf16[8960,3584]{1,0:T(8,128...) custom-call(bf16[7168,3584]{1,0:T(8,128)(2,1)} %l_ref.1, ...), custom_call_target="tpu_custom_call" | custom-call | tf_op jit(solution)/shard_map/triangular_product/pallas_call | solution.py:561
  811.8 20.1 %copy.4 = bf16[7168,2048]{1,0:T(8,128)(2,1)} copy(bf16[7168,2048]{1,0:T(8,128)(2,1)} %get-tuple-element.6) | data formatting | bytes 58720256

commit v5 on v4

--- a/solution.py
+++ b/solution.py
@@ -321,32 +321,6 @@
                      jnp.where(in_a, (r < 5) | (r == 6), n == 0))
         split = is_d & (i == 7)
 
-        @pl.when(first & jnp.logical_not(in_a) & (u == 0))
-        def _():
-            with jax.named_scope('wait_rail'):
-                arrive(k_strip, own)
-
-        @pl.when(first & in_b & split & (u == 2))
-        def _():
-            with jax.named_scope('wait_rail_last'):
-                send_l(l_ref, 7, 7, 8, across, KT, KT).wait_recv()
-                lb_copy(7, KT, KT).start()
-
-        @pl.when(first & jnp.logical_not(mine) & (idx == 0))
-        def _():
-            with jax.named_scope('wait_peer'):
-                @pl.when(in_a)
-                def _():
-                    la_copy(i).wait_recv()
-
-                @pl.when(jnp.logical_not(in_a))
-                def _():
-                    wait_peer(k_strip)
-
-        @pl.when(first & in_b & split & (u == 3))
-        def _():
-            lb_copy(7, KT, KT).wait_recv()
-
         @pl.when(is_a & late & (i == 4) & (n == 0) & (u == 0))
         def _():
             with jax.named_scope('relay'):
@@ -371,6 +345,39 @@
             pltpu.make_async_copy(kept(r, i, n), acc.at[k], psem.at[k]).start()
 
         use_rem = (is_a & late) | (is_c & in_a) | (is_d & in_b) | in_c
+        depth = pl.ds(pl.multiple_of(kt * KT, KT), KT)
+        ncols = pl.ds(pl.multiple_of(n * NT, NT), NT)
+        for take, ref in ((use_rem, brem), (jnp.logical_not(use_rem), b_ref)):
+            @pl.when(take)
+            def _():
+                pltpu.make_async_copy(ref.at[depth, ncols], bt.at[slot], bsem.at[slot]).start()
+
+        @pl.when(first & jnp.logical_not(in_a) & (u == 0))
+        def _():
+            with jax.named_scope('wait_rail'):
+                arrive(k_strip, own)
+
+        @pl.when(first & in_b & split & (u == 2))
+        def _():
+            with jax.named_scope('wait_rail_last'):
+                send_l(l_ref, 7, 7, 8, across, KT, KT).wait_recv()
+                lb_copy(7, KT, KT).start()
+
+        @pl.when(first & jnp.logical_not(mine) & (idx == 0))
+        def _():
+            with jax.named_scope('wait_peer'):
+                @pl.when(in_a)
+                def _():
+                    la_copy(i).wait_recv()
+
+                @pl.when(jnp.logical_not(in_a))
+                def _():
+                    wait_peer(k_strip)
+
+        @pl.when(first & in_b & split & (u == 3))
+        def _():
+            lb_copy(7, KT, KT).wait_recv()
+
         rows = pl.ds(pl.multiple_of(k_strip * S, S), S)
         cols = pl.ds(pl.multiple_of((kt % 2) * KT, KT), KT)
         for take, ref in (
@@ -382,12 +389,6 @@
             @pl.when(take)
             def _():
                 pltpu.make_async_copy(ref.at[rows, cols], lt.at[slot], lsem.at[slot]).start()
-        depth = pl.ds(pl.multiple_of(kt * KT, KT), KT)
-        ncols = pl.ds(pl.multiple_of(n * NT, NT), NT)
-        for take, ref in ((use_rem, brem), (jnp.logical_not(use_rem), b_ref)):
-            @pl.when(take)
-            def _():
-                pltpu.make_async_copy(ref.at[depth, ncols], bt.at[slot], bsem.at[slot]).start()
 
     def finish(r, n):
         late, part, _, i, _, _, _, _, _ = run_of(r)

time: 832 us -> 831 us (level)
  no operation moved by 1% of the time
where the time goes in v5:
time: 831 us
  Pallas kernels  811 us (98%)
  local copies, waits for them, and re-layouts  20.1 us (2%)
    pallas_call x1, Pallas kernels, local_product(): pl.pallas_call(kernel, out_shape=[b_like, l_like, l_more, l_more, b_like,...  811 us
    unnamed x1, local copies, waits for them, and re-layouts  20.1 us

profile of v5, /device:TPU:6, one launch (start us, length us, event | category | flops | bytes accessed | tf_op | source)
XLA Modules:
  0.0 830.9 jit_solution(12306493601835296690)
XLA Ops:
  0.0 810.8 %triangular_product.1 = (bf16[7168,2048]{1,0:T(8,128)(2,1)}, bf16[7168,3584]{1,0:T(8,128)(2,1)}, bf16[8960,3584]{1,0:T(8,128)(2,1)}, bf16[8960,3584]{1,0:T(8,128...) custom-call(bf16[7168,3584]{1,0:T(8,128)(2,1)} %l_ref.1, ...), custom_call_target="tpu_custom_call" | custom-call | tf_op jit(solution)/shard_map/triangular_product/pallas_call | solution.py:562
  810.8 20.1 %copy.4 = bf16[7168,2048]{1,0:T(8,128)(2,1)} copy(bf16[7168,2048]{1,0:T(8,128)(2,1)} %get-tuple-element.6) | data formatting | bytes 58720256
